TPU v7x, 32 devices: a 4x4x1 block of a 4x4x8 slice. The times are simulated.
32 devices in a mesh: dp: 1 (over z), sp: 32 (over x, y, core).
Axes of the slice: x: 4, y: 4, z: 1, core: 2. Of those that a mesh axis runs over, the one named last changes fastest.
The devices are a block of a 4x4x8 slice.
Arguments:
- q: bfloat16 [32, 16, 128], P('dp')
- k: bfloat16 [32, 8192, 16, 128], P('dp', 'sp')
- v: bfloat16 [32, 8192, 16, 128], P('dp', 'sp')
Outputs:
- q: bfloat16 [32, 16, 128], P('dp')
All inputs are finite; a program needn't handle non-finite values.
Results may differ from a plain program's by a relative error of at most 0.012.
Values are sent between devices in bfloat16 or wider.
A program may use at most 768 MiB of HBM per device.

v0:
```python
import jax
import jax.numpy as jnp
from jax import lax
from jax.sharding import PartitionSpec as P


def einsum(form, a, b):
    return jnp.einsum(form, a.astype(jnp.float32), b.astype(jnp.float32))


def part_of(q, k, v):
    grouped = q.reshape(q.shape[0], k.shape[2], -1, q.shape[2])
    scores = einsum("bgsd,bugd->bgsu", grouped, k) * q.shape[2] ** -0.5
    high = jnp.max(scores, -1, keepdims=True)
    weights = jnp.exp(scores - high)
    seen = einsum("bgsu,bugd->bgsd", weights.astype(jnp.bfloat16), v)
    return jnp.concatenate([seen, jnp.sum(weights, -1, keepdims=True), high], -1)


def together(parts):
    seen, total, high = parts[..., :-2], parts[..., -2:-1], parts[..., -1:]
    scale = jnp.exp(high - jnp.max(high, 0))
    return (jnp.sum(seen * scale, 0) / jnp.sum(total * scale, 0)).astype(jnp.bfloat16)


def solution(mesh):
    def step(q, k, v):
        return together(lax.all_gather(part_of(q, k, v), "sp")).reshape(q.shape)

    return jax.shard_map(
        step,
        mesh=mesh,
        in_specs=(P("dp", None, None), P("dp", "sp", None, None), P("dp", "sp", None, None)),
        out_specs=P("dp", None, None),
        check_vma=False,
    )
```

profile of v0, /device:TPU:97, one launch (start us, length us, event | category | flops | bytes accessed | tf_op | source)
XLA Modules:
  0.0 154.1 jit_solution(5927543549171746397)
XLA Ops:
  6.5 0.0 all-gather.3.cloned.1.call-start
  6.6 18.1 %fusion.2 = f32[32,16,1,256]{3,2,1,0:T(1,128)S(1)} fusion(bf16[32,256,16,128]{3,2,1,0:T(8,128)(2,1)} %param.4, bf16[32,16,128,1]{2,1,0,3:T(8,128)(2,1)} %bitcast.25), kind=kOutput, calls=%fused_computation.2 | convolution fusion | flops 33554432 | bytes 34209792 | tf_op jit(solution)/shard_map/bgsd,bugd->bgsu/dot_general | solution.py:8
  24.7 0.1 fusion.9
  24.8 0.3 fusion.10
  25.1 0.3 copy.23
  25.3 0.3 copy.22
  25.6 19.2 %fusion = f32[32,16,1,128]{3,2,1,0:T(1,128)S(1)} fusion(bf16[32,256,16,128]{3,2,1,0:T(8,128)(2,1)} %param.5, bf16[32,16,256,1]{2,1,0,3:T(8,128)(2,1)S(1)} %get-tuple-element.7), kind=kOutput, calls=%fused_computation | convolution fusion | flops 33554432 | bytes 34078720 | tf_op jit(solution)/shard_map/bgsu,bugd->bgsd/dot_general | solution.py:8
  44.8 0.9 pad_maximum_fusion
  45.7 0.1 all-gather.3.cloned.1.call-update
  45.8 71.7 %all-gather.3.cloned.1.call-done = f32[1024,16,1,130]{3,1,2,0:T(8,128)} async-done(((f32[32,16,1,130]{3,1,2,0:T(8,128)}), f32[1024,16,1,130]{3,1,2,0:T(8,128)}) %all-gather.3.cloned.1.call-update) | async-done | bytes 8519696 | tf_op jit(solution)/shard_map/all_gather | solution.py:28
  117.5 5.7 %slice_reduce_fusion = f32[32,16]{1,0:T(8,128)S(1)} fusion(f32[32,32,16,1,130]{4,2,1,0,3:T(8,128)} %bitcast.21), kind=kLoop, calls=%fused_computation.9 | loop fusion | flops 15872 | bytes 67584 | tf_op jit(solution)/shard_map/reduce_max | solution.py:22
  123.2 9.5 %fusion.4 = (f32[32,16]{1,0:T(8,128)S(1)}, f32[32,32,16,1,1]{4,2,1,0,3:T(8,128)}) fusion(f32[32,32,16,1,130]{4,2,1,0,3:T(8,128)} %bitcast.22, f32[32,16]{1,0:T(8,128)S(1)} %slice_reduce_fusion), kind=kLoop, calls=%fused_computation.5 | loop fusion | flops 48640 | bytes 200704 | tf_op jit(solution)/shard_map/reduce_sum | solution.py:23
  132.6 8.4 %copy.36 = f32[32,32,16,1,1]{2,1,0,3,4:T(8,128)S(1)} copy(f32[32,32,16,1,1]{4,2,1,0,3:T(8,128)} %get-tuple-element.6) | data formatting | bytes 131072 | tf_op jit(solution)/shard_map/mul | solution.py:23
  141.1 5.3 %fusion.5 = f32[32,16,128]{2,1,0:T(8,128)S(1)} fusion(f32[32,32,16,1,130]{4,2,1,0,3:T(8,128)} %bitcast.23, f32[32,32,16]{2,1,0:T(8,128)S(1)} %bitcast.24), kind=kLoop, calls=%fused_computation.7 | loop fusion | flops 4128768 | bytes 8716288 | tf_op jit(solution)/shard_map/reduce_sum | solution.py:23
  146.4 0.8 divide_convert_fusion
Async XLA Ops:
  6.5 110.9 %all-gather.3.cloned.1.call-start = ((), (), s32[]{:S(2)}) async-start(), calls=%async_computation | async-start | bytes 17301504 | tf_op jit(solution)/shard_map/all_gather | solution.py:28
Sparse Core Ops, SparseCore 0:
  45.9 71.5 all-gather.2
where the time goes:
time: 154 us
  waiting for transfers between devices  71.7 us (47%)
  matrix products  37.3 us (24%)
  other arithmetic  22.6 us (15%)
  between operations  13.5 us (9%)
  local copies, waits for them, and re-layouts  8.95 us (6%)
    all_gather x1, waiting for transfers between devices, step(): return together(lax.all_gather(part_of(q, k, v), 'sp')).reshape(q.shape)  71.7 us
    dot_general x2, matrix products, einsum(): return jnp.einsum(form, a.astype(jnp.float32), b.astype(jnp.float32))  37.3 us
    reduce_sum x1, other arithmetic, together(): jnp.sum(total * scale, 0)  9.47 us
    mul x1, local copies, waits for them, and re-layouts, together(): seen * scale  8.43 us
    reduce_max x1, other arithmetic, together(): scale = jnp.exp(high - jnp.max(high, 0))  5.69 us
    reduce_sum x1, other arithmetic, together(): jnp.sum(seen * scale, 0) / jnp.sum(total * scale, 0)  5.32 us
  transfers between devices with their start and end apart: 1, of which 1 were waited for; matrix products, arithmetic and copies ran while one was open for 0% of the time, Pallas kernels for 0%

commit v1 on v0

v1 whole, which is shorter than its diff:
```python
import functools

import jax
import jax.numpy as jnp
from jax import lax
from jax.experimental import pallas as pl
from jax.experimental.pallas import tpu as pltpu
from jax.sharding import PartitionSpec as P

MESH = pl.DeviceIdType.MESH
LANES = 128
CORES = 2
SLOTS = 10
GROUP = 4
LAG = 4
LOW = -1e30


def scores(q, k):
    heads = q.shape[0]
    each = LANES // heads
    tiled = jnp.concatenate([q] * each, 0)
    full = lax.dot_general(k, tiled, (((1,), (1,)), ((), ())), preferred_element_type=jnp.float32)
    full = full.reshape(-1, each, heads, LANES)
    lane = lax.broadcasted_iota(jnp.int32, (1, heads, LANES), 2)
    row = lax.broadcasted_iota(jnp.int32, (1, heads, LANES), 1)
    own = full[:, 0]
    for token in range(1, each):
        own = jnp.where(lane // heads == token, full[:, token], own)
    return jnp.where(lane % heads == row, own, LOW)


def kernel(n, q_hbm, k_hbm, v_hbm, o_ref, q_ref, kbuf, vbuf, sbuf, pbuf, o32, o16, m_ref, l_ref, d16, dm, dl, x16, xst, qsem, ksem, vsem, d_send, d_recv, x_send, x_recv, r_send, r_recv):
    N, heads, head = q_ref.shape
    scale = head**-0.5
    half = heads // CORES
    rounds = N // GROUP
    me = lax.axis_index("sp")
    chips = n // CORES
    chip, core = me // CORES, lax.rem(me, CORES)
    other = 1 - core
    partner = chip * CORES + other

    def kcopy(i):
        return pltpu.make_async_copy(k_hbm.at[i], kbuf.at[lax.rem(i, SLOTS)], ksem.at[lax.rem(i, SLOTS)])

    def vcopy(i):
        return pltpu.make_async_copy(v_hbm.at[i], vbuf.at[lax.rem(i, SLOTS)], vsem.at[lax.rem(i, SLOTS)])

    qcopy = pltpu.make_async_copy(q_hbm, q_ref, qsem)
    qcopy.start()
    for i in range(SLOTS + 2):
        if i < SLOTS:
            kcopy(i).start()
        if i >= 2:
            vcopy(i - 2).start()

    barrier = pltpu.get_barrier_semaphore()

    def greet(r, _):
        pl.semaphore_signal(barrier, inc=1, device_id={"sp": lax.rem(chip + r, chips) * CORES + core}, device_id_type=MESH)
        return 0

    lax.fori_loop(1, chips, greet, 0)
    pl.semaphore_signal(barrier, inc=1, device_id={"sp": partner}, device_id_type=MESH)

    def score(i):
        sbuf[lax.rem(i, 2)] = scores(q_ref[i], kbuf[lax.rem(i, SLOTS)])

    def soften(i):
        s = sbuf[lax.rem(i, 2)]
        high = jnp.max(jnp.max(s, 0), -1, keepdims=True)
        w = jnp.exp((s - high[None]) * scale)
        total = jnp.sum(jnp.sum(w, 0), -1, keepdims=True)
        pbuf[lax.rem(i, 2)] = w.astype(jnp.bfloat16)
        m_ref[i] = jnp.broadcast_to(high * scale, (heads, LANES)).reshape(CORES, half, LANES)
        l_ref[i] = jnp.broadcast_to(total, (heads, LANES)).reshape(CORES, half, LANES)

    def weigh(i):
        w = pbuf[lax.rem(i, 2)]
        w = jnp.concatenate([w[b] for b in range(w.shape[0])], 1)
        return jnp.dot(w, vbuf[lax.rem(i, SLOTS)], preferred_element_type=jnp.float32)

    def keep(i, o):
        o = o.reshape(CORES, half, head)
        o32[i] = o
        o16[i] = o.astype(jnp.bfloat16)

    def pair(g):
        run = pl.ds(g * GROUP, GROUP)
        return [
            pltpu.make_async_remote_copy(src.at[run, other], dst.at[run], d_send.at[g, j], d_recv.at[g, j], device_id={"sp": partner}, device_id_type=MESH)
            for j, (src, dst) in enumerate(((o16, d16), (m_ref, dm), (l_ref, dl)))
        ]

    def pair_send(g):
        for copy in pair(g):
            copy.start()

    def spread(g, r):
        to = {"sp": lax.rem(chip + r, chips) * CORES + core}
        return [
            pltpu.make_async_remote_copy(buf.at[g, chip], buf.at[g, chip], x_send.at[g, j], x_recv.at[g, j], device_id=to, device_id_type=MESH)
            for j, buf in enumerate((x16, xst))
        ]

    def chip_send(g):
        for copy in pair(g):
            copy.wait_recv()
        lane = lax.broadcasted_iota(jnp.int32, (half, LANES), 1)
        row = lax.broadcasted_iota(jnp.int32, (half, LANES), 0)
        highs = jnp.zeros((half, LANES), jnp.float32)
        totals = jnp.zeros((half, LANES), jnp.float32)
        for s in range(GROUP):
            i = g * GROUP + s
            m1, m2 = m_ref[i, core], dm[i]
            m = jnp.maximum(m1, m2)
            a1, a2 = jnp.exp(m1 - m), jnp.exp(m2 - m)
            o = o32[i, core] * a1 + d16[i].astype(jnp.float32) * a2
            l = l_ref[i, core] * a1 + dl[i] * a2
            x16[g, chip, s] = o.astype(jnp.bfloat16)
            here = lane == s * half + row
            highs = jnp.where(here, m, highs)
            totals = jnp.where(here, l, totals)
        xst[g, chip] = jnp.concatenate([jnp.sum(highs, 0, keepdims=True), jnp.sum(totals, 0, keepdims=True)], 0)

        def send(r, _):
            for copy in spread(g, r):
                copy.start()
            return 0

        lax.fori_loop(1, chips, send, 0)

    def spread_wait(g, what):
        for j, buf in enumerate((x16, xst)):
            run = buf.at[g, pl.ds(0, chips - 1)]
            pltpu.make_async_copy(run, run, what.at[g, j]).wait()

    def back(g):
        run = pl.ds(g * GROUP, GROUP)
        return pltpu.make_async_remote_copy(o_ref.at[run, core], o_ref.at[run, core], r_send.at[g], r_recv.at[g], device_id={"sp": partner}, device_id_type=MESH)

    def finish(g):
        spread_wait(g, x_recv)
        st = [xst[g, j] for j in range(chips)]
        m = functools.reduce(jnp.maximum, [s[:1] for s in st])
        w = [jnp.exp(s[:1] - m) for s in st]
        total = functools.reduce(jnp.add, [s[1:] * x for s, x in zip(st, w)])
        w = [x / total for x in w]
        lane = lax.broadcasted_iota(jnp.int32, (half, LANES), 1)
        row = lax.broadcasted_iota(jnp.int32, (half, LANES), 0)
        for s in range(GROUP):
            o = jnp.zeros((half, head), jnp.float32)
            for j in range(chips):
                f = jnp.sum(jnp.where(lane == s * half + row, w[j], 0.0), -1, keepdims=True)
                o = o + x16[g, j, s].astype(jnp.float32) * f
            o_ref[g * GROUP + s, core] = o.astype(jnp.bfloat16)
        back(g).start()

    kcopy(0).wait()
    qcopy.wait()
    score(0)
    kcopy(1).wait()
    score(1)
    soften(0)
    pl.semaphore_wait(barrier, chips)

    def refill_k(i):
        @pl.when(i + SLOTS < N)
        def _():
            kcopy(i + SLOTS).start()

    def refill_v(i):
        @pl.when(i + SLOTS < N)
        def _():
            vcopy(i + SLOTS).start()

    refill_k(0)
    refill_k(1)

    def step(i, _):
        kcopy(i + 2).wait()
        vcopy(i).wait()
        s = scores(q_ref[i + 2], kbuf[lax.rem(i + 2, SLOTS)])
        o = weigh(i)
        soften(i + 1)
        sbuf[lax.rem(i, 2)] = s
        keep(i, o)
        refill_k(i + 2)
        refill_v(i)

        @pl.when(lax.rem(i, GROUP) == GROUP - 1)
        def _():
            g = i // GROUP
            pair_send(g)

            @pl.when(g >= 1)
            def _():
                chip_send(g - 1)

            @pl.when(g >= LAG)
            def _():
                finish(g - LAG)

        return 0

    lax.fori_loop(0, N - 2, step, 0)
    vcopy(N - 2).wait()
    o = weigh(N - 2)
    soften(N - 1)
    keep(N - 2, o)
    vcopy(N - 1).wait()
    keep(N - 1, weigh(N - 1))
    last = rounds - 1
    pair_send(last)
    chip_send(last - 1)
    chip_send(last)

    def rest(g, _):
        finish(g)
        return 0

    lax.fori_loop(max((N - 2) // GROUP - LAG, 0), rounds, rest, 0)

    def drain(g, _):
        back(g).wait()
        for copy in pair(g):
            copy.wait_send()
        spread_wait(g, x_send)
        return 0

    lax.fori_loop(0, rounds, drain, 0)


def solution(mesh):
    n = mesh.shape["sp"]

    def step(q, k, v):
        N, tokens, heads, head = k.shape
        half = heads // CORES
        rounds = N // GROUP
        chips = n // CORES
        blocks = tokens * heads // LANES
        flat = (N, tokens * heads, head)
        bf16, f32 = jnp.bfloat16, jnp.float32
        out = pl.pallas_call(
            functools.partial(kernel, n),
            out_shape=jax.ShapeDtypeStruct((N, CORES, half, head), bf16),
            in_specs=[pl.BlockSpec(memory_space=pl.ANY)] * 3,
            out_specs=pl.BlockSpec(memory_space=pltpu.VMEM),
            scratch_shapes=[
                pltpu.VMEM((N, heads, head), bf16),
                pltpu.VMEM((SLOTS, tokens * heads, head), bf16),
                pltpu.VMEM((SLOTS, tokens * heads, head), bf16),
                pltpu.VMEM((2, blocks, heads, LANES), f32),
                pltpu.VMEM((2, blocks, heads, LANES), bf16),
                pltpu.VMEM((N, CORES, half, head), f32),
                pltpu.VMEM((N, CORES, half, head), bf16),
                pltpu.VMEM((N, CORES, half, LANES), f32),
                pltpu.VMEM((N, CORES, half, LANES), f32),
                pltpu.VMEM((N, half, head), bf16),
                pltpu.VMEM((N, half, LANES), f32),
                pltpu.VMEM((N, half, LANES), f32),
                pltpu.VMEM((rounds, chips, GROUP, half, head), bf16),
                pltpu.VMEM((rounds, chips, 2, LANES), f32),
                pltpu.SemaphoreType.DMA(()),
                pltpu.SemaphoreType.DMA((SLOTS,)),
                pltpu.SemaphoreType.DMA((SLOTS,)),
                pltpu.SemaphoreType.DMA((rounds, 3)),
                pltpu.SemaphoreType.DMA((rounds, 3)),
                pltpu.SemaphoreType.DMA((rounds, 2)),
                pltpu.SemaphoreType.DMA((rounds, 2)),
                pltpu.SemaphoreType.DMA((rounds,)),
                pltpu.SemaphoreType.DMA((rounds,)),
            ],
            compiler_params=pltpu.CompilerParams(collective_id=0, has_side_effects=True, vmem_limit_bytes=60 * 2**20),
        )(q, k.reshape(flat), v.reshape(flat))
        return out.reshape(q.shape)

    return jax.shard_map(
        step,
        mesh=mesh,
        in_specs=(P("dp", None, None), P("dp", "sp", None, None), P("dp", "sp", None, None)),
        out_specs=P("dp", None, None),
        check_vma=False,
    )
```

time: 154 us -> 49.1 us (0.32)
  waiting for transfers between devices: 71.7 us -> 0 us
  Pallas kernels: 0 us -> 47.5 us
  matrix products: 37.3 us -> 0 us
  other arithmetic: 22.6 us -> 0 us
  between operations: 13.5 us -> 0.01 us
  local copies, waits for them, and re-layouts: 8.95 us -> 1.57 us
    all_gather x1 -> x0, waiting for transfers between devices: 71.7 us -> none  [step(): return together(lax.all_gather(part_of(q, k, v), 'sp')).reshape(q.shape)]
    pallas_call x0 -> x1, Pallas kernels: none -> 47.5 us  [step(): pl.pallas_call(functools.partial(kernel, n), out_shape=jax.ShapeDtypeStru...]
    dot_general x2 -> x0, matrix products: 37.3 us -> none  [einsum(): return jnp.einsum(form, a.astype(jnp.float32), b.astype(jnp.float32))]
    reduce_sum x2 -> x0, other arithmetic: 14.8 us -> none  [the longest x1 9.47 us: together(): jnp.sum(total * scale, 0)]
    mul x1 -> x0, local copies, waits for them, and re-layouts: 8.43 us -> none  [together(): seen * scale]
    reduce_max x2 -> x0, other arithmetic: 5.84 us -> none  [the longest x1 5.69 us: together(): scale = jnp.exp(high - jnp.max(high, 0))]
    unnamed x0 -> x1, local copies, waits for them, and re-layouts: none -> 1.57 us
  transfers between devices with their start and end apart: 1 -> 0, of which waited for: 1 -> 0; matrix products, arithmetic and copies ran while one was open for 0% -> 0% of each run, Pallas kernels for 0% -> 0%
where the time goes in v1:
time: 49.1 us; the launch traced here: 49 us
  Pallas kernels  47.5 us (97%)
  local copies, waits for them, and re-layouts  1.57 us (3%)
    pallas_call x1, Pallas kernels, step(): pl.pallas_call(functools.partial(kernel, n), out_shape=jax.ShapeDtypeStru...  47.5 us
    unnamed x1, local copies, waits for them, and re-layouts  1.57 us

profile of v1, /device:TPU:97, one launch (start us, length us, event | category | flops | bytes accessed | tf_op | source)
XLA Modules:
  0.0 49.0 jit_solution(5465201876235463043)
XLA Ops:
  0.0 47.5 %shard_map.37 = bf16[32,2,8,128]{3,2,1,0:T(8,128)(2,1)} custom-call(bf16[32,16,128]{2,1,0:T(8,128)(2,1)} %q_hbm.1, bf16[32,4096,128]{2,1,0:T(8,128)(2,1)} %bitcast.3, bf16[32,4096,128]{2,1,0:T(8,128)(2,1)} %bitcast.4), custom_call_target="tpu_custom_call" | custom-call | tf_op jit(solution)/shard_map/pallas_call | solution.py:246
  47.5 1.6 %copy.5 = bf16[32,16,128]{2,1,0:T(8,128)(2,1)} copy(bf16[32,16,128]{2,1,0:T(8,128)(2,1)} %bitcast.5) | data formatting | bytes 262144

commit v2 on v0

v2 whole, which is shorter than its diff:
```python
import functools

import jax
import jax.numpy as jnp
from jax import lax
from jax.experimental import pallas as pl
from jax.experimental.pallas import tpu as pltpu
from jax.sharding import PartitionSpec as P

MESH = pl.DeviceIdType.MESH
LANES, ROWS = 128, 8
SLOTS = 8
STEP = 2
LAST = 4
HOLD = 12
LOW = -1e30
ABL = 0
AHEAD = 6


def kernel(n, q_hbm, k_hbm, v_hbm, o_ref, q_ref, kbuf, vbuf, sbuf, pbuf, st_ref, msg, inbox, x16, xst, qsem, ksem, vsem, p_send, p_recv, b_send, b_recv, x_send, x_recv):
    N, heads, head = q_ref.shape
    scale = head**-0.5
    halves = heads // ROWS
    owned = N - LAST
    me = lax.axis_index("sp")

    def kcopy(i):
        return pltpu.make_async_copy(k_hbm.at[i], kbuf.at[lax.rem(i, SLOTS)], ksem.at[lax.rem(i, SLOTS)])

    def vcopy(i):
        return pltpu.make_async_copy(v_hbm.at[i], vbuf.at[lax.rem(i, SLOTS)], vsem.at[lax.rem(i, SLOTS)])

    qcopy = pltpu.make_async_copy(q_hbm, q_ref, qsem)
    qcopy.start(priority=1)
    first = [kcopy(i) for i in range(2 * STEP)]
    for i in range(SLOTS):
        first.append(vcopy(i))
        if i + 2 * STEP < SLOTS:
            first.append(kcopy(i + 2 * STEP))
    for copy in first[:AHEAD]:
        copy.start(priority=1)

    barrier = pltpu.get_barrier_semaphore()

    def peer(r):
        return {"sp": lax.rem(me + r, n)}

    def greet(r, _):
        pl.semaphore_signal(barrier, inc=1, device_id=peer(r), device_id_type=MESH)
        return 0

    lax.fori_loop(1, n, greet, 0)

    lane = lax.broadcasted_iota(jnp.int32, (ROWS, LANES), 1)
    each = LANES // 2 // halves

    def score(i):
        return lax.dot_general(q_ref[i], kbuf[lax.rem(i, SLOTS)], (((1,), (1,)), ((), ())), preferred_element_type=jnp.float32)

    def soften(i):
        s = sbuf[lax.rem(i, 2 * STEP)]
        places = lax.broadcasted_iota(jnp.int32, s.shape, 1)
        rows = lax.broadcasted_iota(jnp.int32, s.shape, 0)
        s = jnp.where(places % heads == rows, s, LOW)
        high = jnp.max(s, -1, keepdims=True)
        w = jnp.exp((s - high) * scale)
        total = jnp.sum(w, -1, keepdims=True)
        pbuf[lax.rem(i, 2 * STEP)] = w.astype(jnp.bfloat16)
        tile = jnp.zeros((ROWS, LANES), jnp.float32)
        for h in range(halves):
            run = slice(h * ROWS, (h + 1) * ROWS)
            tile = jnp.where(lane == h * each, high[run] * scale, tile)
            tile = jnp.where(lane == LANES // 2 + h * each, total[run], tile)
        st_ref[i] = tile

    def weigh(i):
        return jnp.dot(pbuf[lax.rem(i, 2 * STEP)], vbuf[lax.rem(i, SLOTS)], preferred_element_type=jnp.float32)

    def keep(i, o):
        msg[i, :halves] = o.reshape(halves, ROWS, head)
        msg[i, halves] = st_ref[i]

    def keep_last(i, o):
        x16[me, i - owned] = o.reshape(halves, ROWS, head).astype(jnp.bfloat16)
        here = st_ref[i] if i == owned else pltpu.roll(st_ref[i], i - owned, 1)
        xst[me] = here if i == owned else jnp.where(lane % each == i - owned, here, xst[me])

    def merge(count, part, tiles):
        high = functools.reduce(jnp.maximum, tiles)
        ws = [jnp.exp(t - high) for t in tiles]
        total = functools.reduce(jnp.add, [pltpu.roll(t, LANES // 2, 1) * w for t, w in zip(tiles, ws)])
        fs = [w / total for w in ws]
        return [
            jnp.stack([functools.reduce(jnp.add, [part(j, s, h).astype(jnp.float32) * f[:, h * each + s : h * each + s + 1] for j, f in enumerate(fs)]) for h in range(halves)])
            for s in range(count)
        ]

    def to_owner(i):
        return pltpu.make_async_remote_copy(msg.at[i], inbox.at[me], p_send.at[i], p_recv, device_id={"sp": i}, device_id_type=MESH)

    def send_part(i):
        @pl.when(i != me)
        def _():
            to_owner(i).start()

    def spread(ref, sem, j):
        return lambda r: pltpu.make_async_remote_copy(ref, ref, x_send.at[j], sem, device_id=peer(r), device_id_type=MESH)

    def all_of(ref, sem):
        run = ref.at[pl.ds(0, n - 1)]
        pltpu.make_async_copy(run, run, sem).wait()

    def result_copy(r):
        return pltpu.make_async_remote_copy(o_ref.at[me], o_ref.at[me], b_send, b_recv.at[me], device_id=peer(r), device_id_type=MESH)

    def own():
        inbox[me] = msg[me]
        all_of(inbox, p_recv)
        o_ref[me] = merge(1, lambda j, s, h: inbox[j, h], [inbox[j, halves] for j in range(n)])[0].astype(jnp.bfloat16)

        def send(r, _):
            result_copy(r).start()
            return 0

        lax.fori_loop(1, n, send, 0)

    for i in range(2 * STEP):
        kcopy(i).wait()
        if i == 0:
            qcopy.wait()
        rest = len(first) - AHEAD
        for copy in first[AHEAD + rest * i // (2 * STEP) : AHEAD + rest * (i + 1) // (2 * STEP)]:
            copy.start(priority=1)
        sbuf[i] = score(i)
        if i < STEP:
            soften(i)

    def refill(copy, i):
        @pl.when(i + SLOTS < N)
        def _():
            copy(i + SLOTS).start(priority=1)

    for i in range(2 * STEP):
        refill(kcopy, i)

    def step(t, _):
        i = t * STEP
        for u in range(STEP):
            kcopy(i + 2 * STEP + u).wait()
            vcopy(i + u).wait()
        os = [weigh(i + u) for u in range(STEP)]
        ss = [score(i + 2 * STEP + u) for u in range(STEP)]
        for u in range(STEP):
            soften(i + STEP + u)
        for u in range(STEP):
            sbuf[lax.rem(i + u, 2 * STEP)] = ss[u]
            keep(i + u, os[u])
        for u in range(STEP):
            refill(kcopy, i + 2 * STEP + u)
            refill(vcopy, i + u)
        if ABL:
            return 0

        @pl.when(i == HOLD)
        def _():
            pl.semaphore_wait(barrier, n - 1)

            def send(j, _):
                send_part(j)
                return 0

            lax.fori_loop(0, HOLD, send, 0)

        @pl.when(i >= HOLD)
        def _():
            for u in range(STEP):
                send_part(i + u)

        return 0

    lax.fori_loop(0, (N - 2 * STEP) // STEP, step, 0)
    for i in range(N - 2 * STEP, N):
        if i < N - STEP:
            soften(i + STEP)
        vcopy(i).wait()
        o = weigh(i)
        if i < owned:
            keep(i, o)
            if not ABL:
                send_part(i)
        else:
            keep_last(i, o)
    if ABL:
        pl.semaphore_wait(barrier, n - 1)
        return

    def send_last(r, _):
        for j, (ref, sem) in enumerate(((x16.at[me], x_recv.at[0]), (xst.at[me], x_recv.at[1]))):
            spread(ref, sem, j)(r).start()
        return 0

    lax.fori_loop(1, n, send_last, 0)
    pl.when(me < owned)(own)
    all_of(x16, x_recv.at[0])
    all_of(xst, x_recv.at[1])
    for s, o in enumerate(merge(LAST, lambda j, s, h: x16[j, s, h], [xst[j] for j in range(n)])):
        o_ref[owned + s] = o.astype(jnp.bfloat16)

    def drain(i, _):
        @pl.when(i != me)
        def _():
            to_owner(i).wait_send()
            pltpu.make_async_copy(o_ref.at[i], o_ref.at[i], b_recv.at[i]).wait()

        return 0

    lax.fori_loop(0, owned, drain, 0)

    @pl.when(me < owned)
    def _():
        all_of(o_ref, b_send)

    all_of(x16, x_send.at[0])
    all_of(xst, x_send.at[1])


def solution(mesh):
    n = mesh.shape["sp"]

    def step(q, k, v):
        N, tokens, heads, head = k.shape
        halves = heads // ROWS
        flat = (N, tokens * heads, head)
        bf16, f32 = jnp.bfloat16, jnp.float32
        dma = pltpu.SemaphoreType.DMA
        out = pl.pallas_call(
            functools.partial(kernel, n),
            out_shape=pltpu.VMEM((N, halves, ROWS, head), bf16),
            in_specs=[pl.BlockSpec(memory_space=pl.ANY)] * 3,
            out_specs=pl.BlockSpec(memory_space=pltpu.VMEM),
            scratch_shapes=[
                pltpu.VMEM((N, heads, head), bf16),
                pltpu.VMEM((SLOTS, tokens * heads, head), bf16),
                pltpu.VMEM((SLOTS, tokens * heads, head), bf16),
                pltpu.VMEM((2 * STEP, heads, tokens * heads), f32),
                pltpu.VMEM((2 * STEP, heads, tokens * heads), bf16),
                pltpu.VMEM((N, ROWS, LANES), f32),
                pltpu.VMEM((N, halves + 1, ROWS, LANES), f32),
                pltpu.VMEM((n, halves + 1, ROWS, LANES), f32),
                pltpu.VMEM((n, LAST, halves, ROWS, head), bf16),
                pltpu.VMEM((n, ROWS, LANES), f32),
                dma(()),
                dma((SLOTS,)),
                dma((SLOTS,)),
                dma((N,)),
                dma(()),
                dma(()),
                dma((N,)),
                dma((2,)),
                dma((2,)),
            ],
            compiler_params=pltpu.CompilerParams(collective_id=0, has_side_effects=True, vmem_limit_bytes=60 * 2**20),
        )(q, k.reshape(flat), v.reshape(flat))
        return out.reshape(q.shape)

    return jax.shard_map(
        step,
        mesh=mesh,
        in_specs=(P("dp", None, None), P("dp", "sp", None, None), P("dp", "sp", None, None)),
        out_specs=P("dp", None, None),
        check_vma=False,
    )
```

time: 154 us -> 40.9 us (0.27)
  waiting for transfers between devices: 71.7 us -> 0 us
  Pallas kernels: 0 us -> 40.1 us
  matrix products: 37.3 us -> 0 us
  other arithmetic: 22.6 us -> 0 us
  between operations: 13.5 us -> 0.01 us
  local copies, waits for them, and re-layouts: 8.95 us -> 0.66 us
    all_gather x1 -> x0, waiting for transfers between devices: 71.7 us -> none  [step(): return together(lax.all_gather(part_of(q, k, v), 'sp')).reshape(q.shape)]
    pallas_call x0 -> x1, Pallas kernels: none -> 40.1 us  [step(): pl.pallas_call(functools.partial(kernel, n), out_shape=pltpu.VMEM((N, hal...]
    dot_general x2 -> x0, matrix products: 37.3 us -> none  [einsum(): return jnp.einsum(form, a.astype(jnp.float32), b.astype(jnp.float32))]
    reduce_sum x2 -> x0, other arithmetic: 14.8 us -> none  [the longest x1 9.47 us: together(): jnp.sum(total * scale, 0)]
    mul x1 -> x0, local copies, waits for them, and re-layouts: 8.43 us -> none  [together(): seen * scale]
    reduce_max x2 -> x0, other arithmetic: 5.84 us -> none  [the longest x1 5.69 us: together(): scale = jnp.exp(high - jnp.max(high, 0))]
  transfers between devices with their start and end apart: 1 -> 0, of which waited for: 1 -> 0; matrix products, arithmetic and copies ran while one was open for 0% -> 0% of each run, Pallas kernels for 0% -> 0%
where the time goes in v2:
time: 40.9 us; the launch traced here: 40.8 us
  Pallas kernels  40.1 us (98%)
  local copies, waits for them, and re-layouts  0.66 us (2%)
    pallas_call x1, Pallas kernels, step(): pl.pallas_call(functools.partial(kernel, n), out_shape=pltpu.VMEM((N, hal...  40.1 us

profile of v2, /device:TPU:97, one launch (start us, length us, event | category | flops | bytes accessed | tf_op | source)
XLA Modules:
  0.0 40.8 jit_solution(10163664418152798891)
XLA Ops:
  0.0 40.1 %shard_map.37 = bf16[32,2,8,128]{3,2,1,0:T(8,128)(2,1)S(1)} custom-call(bf16[32,16,128]{2,1,0:T(8,128)(2,1)} %q_hbm.1, bf16[32,4096,128]{2,1,0:T(8,128)(2,1)} %bitcast.4, bf16[32,4096,128]{2,1,0:T(8,128)(2,1)} %bitcast.5), custom_call_target="tpu_custom_call" | custom-call | tf_op jit(solution)/shard_map/pallas_call | solution.py:237
  40.1 0.7 %copy.5 = bf16[32,16,128]{2,1,0:T(8,128)(2,1)} copy(bf16[32,16,128]{2,1,0:T(8,128)(2,1)S(1)} %bitcast.3) | data formatting | bytes 262144

commit v3 on v2

--- a/solution.py
+++ b/solution.py
@@ -9,12 +9,12 @@
 
 MESH = pl.DeviceIdType.MESH
 LANES, ROWS = 128, 8
-SLOTS = 8
+KEYS, SLOTS = 8, 8
 STEP = 2
-LAST = 4
+LAST = 3
 HOLD = 12
 LOW = -1e30
-ABL = 0
+LEAD = 4
 AHEAD = 6
 
 
@@ -26,25 +26,26 @@
     me = lax.axis_index("sp")
 
     def kcopy(i):
-        return pltpu.make_async_copy(k_hbm.at[i], kbuf.at[lax.rem(i, SLOTS)], ksem.at[lax.rem(i, SLOTS)])
+        return pltpu.make_async_copy(k_hbm.at[i], kbuf.at[lax.rem(i, KEYS)], ksem.at[lax.rem(i, KEYS)])
 
     def vcopy(i):
         return pltpu.make_async_copy(v_hbm.at[i], vbuf.at[lax.rem(i, SLOTS)], vsem.at[lax.rem(i, SLOTS)])
 
     qcopy = pltpu.make_async_copy(q_hbm, q_ref, qsem)
     qcopy.start(priority=1)
-    first = [kcopy(i) for i in range(2 * STEP)]
-    for i in range(SLOTS):
-        first.append(vcopy(i))
-        if i + 2 * STEP < SLOTS:
-            first.append(kcopy(i + 2 * STEP))
+    first = [kcopy(i) for i in range(LEAD)]
+    for i in range(max(SLOTS, KEYS - LEAD)):
+        if i < SLOTS:
+            first.append(vcopy(i))
+        if i + LEAD < KEYS:
+            first.append(kcopy(i + LEAD))
     for copy in first[:AHEAD]:
         copy.start(priority=1)
 
     barrier = pltpu.get_barrier_semaphore()
 
     def peer(r):
-        return {"sp": lax.rem(me + r, n)}
+        return {"sp": r - 1 + jnp.where(r > me, 1, 0)}
 
     def greet(r, _):
         pl.semaphore_signal(barrier, inc=1, device_id=peer(r), device_id_type=MESH)
@@ -56,7 +57,7 @@
     each = LANES // 2 // halves
 
     def score(i):
-        return lax.dot_general(q_ref[i], kbuf[lax.rem(i, SLOTS)], (((1,), (1,)), ((), ())), preferred_element_type=jnp.float32)
+        return lax.dot_general(q_ref[i], kbuf[lax.rem(i, KEYS)], (((1,), (1,)), ((), ())), preferred_element_type=jnp.float32)
 
     def soften(i):
         s = sbuf[lax.rem(i, 2 * STEP)]
@@ -66,7 +67,7 @@
         high = jnp.max(s, -1, keepdims=True)
         w = jnp.exp((s - high) * scale)
         total = jnp.sum(w, -1, keepdims=True)
-        pbuf[lax.rem(i, 2 * STEP)] = w.astype(jnp.bfloat16)
+        pbuf[lax.rem(i, LEAD)] = w.astype(jnp.bfloat16)
         tile = jnp.zeros((ROWS, LANES), jnp.float32)
         for h in range(halves):
             run = slice(h * ROWS, (h + 1) * ROWS)
@@ -75,7 +76,7 @@
         st_ref[i] = tile
 
     def weigh(i):
-        return jnp.dot(pbuf[lax.rem(i, 2 * STEP)], vbuf[lax.rem(i, SLOTS)], preferred_element_type=jnp.float32)
+        return jnp.dot(pbuf[lax.rem(i, LEAD)], vbuf[lax.rem(i, SLOTS)], preferred_element_type=jnp.float32)
 
     def keep(i, o):
         msg[i, :halves] = o.reshape(halves, ROWS, head)
@@ -97,7 +98,7 @@
         ]
 
     def to_owner(i):
-        return pltpu.make_async_remote_copy(msg.at[i], inbox.at[me], p_send.at[i], p_recv, device_id={"sp": i}, device_id_type=MESH)
+        return pltpu.make_async_remote_copy(msg.at[i], inbox.at[me], p_send, p_recv, device_id={"sp": i}, device_id_type=MESH)
 
     def send_part(i):
         @pl.when(i != me)
@@ -112,7 +113,7 @@
         pltpu.make_async_copy(run, run, sem).wait()
 
     def result_copy(r):
-        return pltpu.make_async_remote_copy(o_ref.at[me], o_ref.at[me], b_send, b_recv.at[me], device_id=peer(r), device_id_type=MESH)
+        return pltpu.make_async_remote_copy(o_ref.at[me], o_ref.at[me], b_send, b_recv, device_id=peer(r), device_id_type=MESH)
 
     def own():
         inbox[me] = msg[me]
@@ -125,42 +126,56 @@
 
         lax.fori_loop(1, n, send, 0)
 
-    for i in range(2 * STEP):
-        kcopy(i).wait()
-        if i == 0:
-            qcopy.wait()
-        rest = len(first) - AHEAD
-        for copy in first[AHEAD + rest * i // (2 * STEP) : AHEAD + rest * (i + 1) // (2 * STEP)]:
-            copy.start(priority=1)
-        sbuf[i] = score(i)
-        if i < STEP:
-            soften(i)
-
-    def refill(copy, i):
-        @pl.when(i + SLOTS < N)
-        def _():
-            copy(i + SLOTS).start(priority=1)
-
-    for i in range(2 * STEP):
-        refill(kcopy, i)
+    def refill(copy, i, slots):
+        @pl.when(i + slots < N)
+        def _():
+            copy(i + slots).start(priority=1)
+
+    def score_step(i):
+        for u in range(STEP):
+            kcopy(i + u).wait()
+        return [score(i + u) for u in range(STEP)]
+
+    def hold(i, ss):
+        for u in range(STEP):
+            sbuf[lax.rem(i + u, 2 * STEP)] = ss[u]
+
+    kcopy(0).wait()
+    qcopy.wait()
+    for copy in first[AHEAD:]:
+        copy.start(priority=1)
+    kcopy(1).wait()
+    hold(0, [score(u) for u in range(STEP)])
+
+    def early(t, _):
+        i = t * STEP
+        ss = score_step(i)
+        for u in range(STEP):
+            soften(i - STEP + u)
+        hold(i, ss)
+        for u in range(STEP):
+            refill(kcopy, i - STEP + u, KEYS)
+        return 0
+
+    lax.fori_loop(1, LEAD // STEP, early, 0)
+    for u in range(STEP):
+        refill(kcopy, LEAD - STEP + u, KEYS)
 
     def step(t, _):
         i = t * STEP
         for u in range(STEP):
-            kcopy(i + 2 * STEP + u).wait()
+            kcopy(i + LEAD + u).wait()
             vcopy(i + u).wait()
         os = [weigh(i + u) for u in range(STEP)]
-        ss = [score(i + 2 * STEP + u) for u in range(STEP)]
-        for u in range(STEP):
-            soften(i + STEP + u)
-        for u in range(STEP):
-            sbuf[lax.rem(i + u, 2 * STEP)] = ss[u]
+        ss = [score(i + LEAD + u) for u in range(STEP)]
+        for u in range(STEP):
+            soften(i + LEAD - STEP + u)
+        hold(i + LEAD, ss)
+        for u in range(STEP):
             keep(i + u, os[u])
         for u in range(STEP):
-            refill(kcopy, i + 2 * STEP + u)
-            refill(vcopy, i + u)
-        if ABL:
-            return 0
+            refill(kcopy, i + LEAD + u, KEYS)
+            refill(vcopy, i + u, SLOTS)
 
         @pl.when(i == HOLD)
         def _():
@@ -179,21 +194,24 @@
 
         return 0
 
-    lax.fori_loop(0, (N - 2 * STEP) // STEP, step, 0)
-    for i in range(N - 2 * STEP, N):
-        if i < N - STEP:
-            soften(i + STEP)
-        vcopy(i).wait()
-        o = weigh(i)
-        if i < owned:
-            keep(i, o)
-            if not ABL:
-                send_part(i)
-        else:
-            keep_last(i, o)
-    if ABL:
-        pl.semaphore_wait(barrier, n - 1)
-        return
+    lax.fori_loop(0, (N - LEAD) // STEP, step, 0)
+    for i in range(N - LEAD, N, STEP):
+        pairs = [range(i, i + STEP)] if i + STEP < N else [range(u, u + 1) for u in range(i, N)]
+        for pair in pairs:
+            for u in pair:
+                vcopy(u).wait()
+            os = [weigh(u) for u in pair]
+            if i == N - LEAD:
+                for u in range(STEP):
+                    soften(N - STEP + u)
+            for u, o in zip(pair, os):
+                if u < owned:
+                    keep(u, o)
+                else:
+                    keep_last(u, o)
+            for u in pair:
+                if u < owned:
+                    send_part(u)
 
     def send_last(r, _):
         for j, (ref, sem) in enumerate(((x16.at[me], x_recv.at[0]), (xst.at[me], x_recv.at[1]))):
@@ -207,19 +225,20 @@
     for s, o in enumerate(merge(LAST, lambda j, s, h: x16[j, s, h], [xst[j] for j in range(n)])):
         o_ref[owned + s] = o.astype(jnp.bfloat16)
 
-    def drain(i, _):
-        @pl.when(i != me)
-        def _():
-            to_owner(i).wait_send()
-            pltpu.make_async_copy(o_ref.at[i], o_ref.at[i], b_recv.at[i]).wait()
-
-        return 0
-
-    lax.fori_loop(0, owned, drain, 0)
+    def blocks(ref, count, sem):
+        run = ref.at[pl.ds(0, count)]
+        pltpu.make_async_copy(run, run, sem).wait()
 
     @pl.when(me < owned)
     def _():
-        all_of(o_ref, b_send)
+        blocks(o_ref, n - 1, b_send)
+        blocks(o_ref, owned - 1, b_recv)
+        blocks(msg, owned - 1, p_send)
+
+    @pl.when(me >= owned)
+    def _():
+        blocks(o_ref, owned, b_recv)
+        blocks(msg, owned, p_send)
 
     all_of(x16, x_send.at[0])
     all_of(xst, x_send.at[1])
@@ -241,22 +260,19 @@
             out_specs=pl.BlockSpec(memory_space=pltpu.VMEM),
             scratch_shapes=[
                 pltpu.VMEM((N, heads, head), bf16),
-                pltpu.VMEM((SLOTS, tokens * heads, head), bf16),
+                pltpu.VMEM((KEYS, tokens * heads, head), bf16),
                 pltpu.VMEM((SLOTS, tokens * heads, head), bf16),
                 pltpu.VMEM((2 * STEP, heads, tokens * heads), f32),
-                pltpu.VMEM((2 * STEP, heads, tokens * heads), bf16),
+                pltpu.VMEM((LEAD, heads, tokens * heads), bf16),
                 pltpu.VMEM((N, ROWS, LANES), f32),
                 pltpu.VMEM((N, halves + 1, ROWS, LANES), f32),
                 pltpu.VMEM((n, halves + 1, ROWS, LANES), f32),
                 pltpu.VMEM((n, LAST, halves, ROWS, head), bf16),
                 pltpu.VMEM((n, ROWS, LANES), f32),
                 dma(()),
+                dma((KEYS,)),
                 dma((SLOTS,)),
-                dma((SLOTS,)),
-                dma((N,)),
-                dma(()),
-                dma(()),
-                dma((N,)),
+                *[dma(())] * 4,
                 dma((2,)),
                 dma((2,)),
             ],

time: 40.9 us -> 38.1 us (0.932)
  Pallas kernels: 40.1 us -> 37.3 us
    pallas_call x1, Pallas kernels: 40.1 us -> 37.3 us  [step(): pl.pallas_call(functools.partial(kernel, n), out_shape=pltpu.VMEM((N, hal...]
where the time goes in v3:
time: 38.1 us; the launch traced here: 38 us
  Pallas kernels  37.3 us (98%)
  local copies, waits for them, and re-layouts  0.66 us (2%)
    pallas_call x1, Pallas kernels, step(): pl.pallas_call(functools.partial(kernel, n), out_shape=pltpu.VMEM((N, hal...  37.3 us

profile of v3, /device:TPU:97, one launch (start us, length us, event | category | flops | bytes accessed | tf_op | source)
XLA Modules:
  0.0 38.0 jit_solution(9484344293186875812)
XLA Ops:
  0.0 37.3 %shard_map.37 = bf16[32,2,8,128]{3,2,1,0:T(8,128)(2,1)S(1)} custom-call(bf16[32,16,128]{2,1,0:T(8,128)(2,1)} %q_hbm.1, bf16[32,4096,128]{2,1,0:T(8,128)(2,1)} %bitcast.4, bf16[32,4096,128]{2,1,0:T(8,128)(2,1)} %bitcast.5), custom_call_target="tpu_custom_call" | custom-call | tf_op jit(solution)/shard_map/pallas_call | solution.py:256
  37.4 0.7 %copy.5 = bf16[32,16,128]{2,1,0:T(8,128)(2,1)} copy(bf16[32,16,128]{2,1,0:T(8,128)(2,1)S(1)} %bitcast.3) | data formatting | bytes 262144

commit v4 on v3

--- a/solution.py
+++ b/solution.py
@@ -18,7 +18,7 @@
 AHEAD = 6
 
 
-def kernel(n, q_hbm, k_hbm, v_hbm, o_ref, q_ref, kbuf, vbuf, sbuf, pbuf, st_ref, msg, inbox, x16, xst, qsem, ksem, vsem, p_send, p_recv, b_send, b_recv, x_send, x_recv):
+def kernel(n, q_hbm, k_hbm, v_hbm, o_ref, q_ref, kbuf, vbuf, sbuf, pbuf, st_ref, msg, inbox, x16, xst, factor, qsem, ksem, vsem, p_send, p_recv, b_send, b_recv, x_send, x_recv):
     N, heads, head = q_ref.shape
     scale = head**-0.5
     halves = heads // ROWS
@@ -84,18 +84,37 @@
 
     def keep_last(i, o):
         x16[me, i - owned] = o.reshape(halves, ROWS, head).astype(jnp.bfloat16)
-        here = st_ref[i] if i == owned else pltpu.roll(st_ref[i], i - owned, 1)
-        xst[me] = here if i == owned else jnp.where(lane % each == i - owned, here, xst[me])
-
-    def merge(count, part, tiles):
+
+    def pack_last():
+        tile = st_ref[owned]
+        for s in range(1, LAST):
+            tile = jnp.where(lane % each == s, pltpu.roll(st_ref[owned + s], s, 1), tile)
+        xst[me] = tile
+
+    def shares(tiles):
         high = functools.reduce(jnp.maximum, tiles)
         ws = [jnp.exp(t - high) for t in tiles]
         total = functools.reduce(jnp.add, [pltpu.roll(t, LANES // 2, 1) * w for t, w in zip(tiles, ws)])
-        fs = [w / total for w in ws]
-        return [
-            jnp.stack([functools.reduce(jnp.add, [part(j, s, h).astype(jnp.float32) * f[:, h * each + s : h * each + s + 1] for j, f in enumerate(fs)]) for h in range(halves)])
-            for s in range(count)
-        ]
+        return [w / total for w in ws]
+
+    def merge_own():
+        fs = shares([inbox[j, halves] for j in range(n)])
+        for h in range(halves):
+            o = functools.reduce(jnp.add, [inbox[j, h] * f[:, h * each : h * each + 1] for j, f in enumerate(fs)])
+            o_ref[me, h] = o.astype(jnp.bfloat16)
+
+    def shares_last():
+        for j, f in enumerate(shares([xst[j] for j in range(n)])):
+            for s in range(LAST):
+                for h in range(halves):
+                    at = h * each + s
+                    factor[j, s, h] = jnp.broadcast_to(f[:, at : at + 1], (ROWS, LANES))
+
+    def merge_last():
+        for s in range(LAST):
+            for h in range(halves):
+                o = functools.reduce(jnp.add, [x16[j, s, h].astype(jnp.float32) * factor[j, s, h] for j in range(n)])
+                o_ref[owned + s, h] = o.astype(jnp.bfloat16)
 
     def to_owner(i):
         return pltpu.make_async_remote_copy(msg.at[i], inbox.at[me], p_send, p_recv, device_id={"sp": i}, device_id_type=MESH)
@@ -105,8 +124,12 @@
         def _():
             to_owner(i).start()
 
-    def spread(ref, sem, j):
-        return lambda r: pltpu.make_async_remote_copy(ref, ref, x_send.at[j], sem, device_id=peer(r), device_id_type=MESH)
+    def spread(ref, j):
+        def send(r, _):
+            pltpu.make_async_remote_copy(ref.at[me], ref.at[me], x_send.at[j], x_recv.at[j], device_id=peer(r), device_id_type=MESH).start()
+            return 0
+
+        lax.fori_loop(1, n, send, 0)
 
     def all_of(ref, sem):
         run = ref.at[pl.ds(0, n - 1)]
@@ -118,7 +141,7 @@
     def own():
         inbox[me] = msg[me]
         all_of(inbox, p_recv)
-        o_ref[me] = merge(1, lambda j, s, h: inbox[j, h], [inbox[j, halves] for j in range(n)])[0].astype(jnp.bfloat16)
+        merge_own()
 
         def send(r, _):
             result_copy(r).start()
@@ -196,14 +219,15 @@
 
     lax.fori_loop(0, (N - LEAD) // STEP, step, 0)
     for i in range(N - LEAD, N, STEP):
-        pairs = [range(i, i + STEP)] if i + STEP < N else [range(u, u + 1) for u in range(i, N)]
+        pairs = [range(i, i + STEP)] if i + STEP <= owned else [range(u, u + 1) for u in range(i, i + STEP)]
         for pair in pairs:
             for u in pair:
                 vcopy(u).wait()
             os = [weigh(u) for u in pair]
-            if i == N - LEAD:
+            if pair[0] == N - LEAD:
                 for u in range(STEP):
                     soften(N - STEP + u)
+                pack_last()
             for u, o in zip(pair, os):
                 if u < owned:
                     keep(u, o)
@@ -212,18 +236,15 @@
             for u in pair:
                 if u < owned:
                     send_part(u)
-
-    def send_last(r, _):
-        for j, (ref, sem) in enumerate(((x16.at[me], x_recv.at[0]), (xst.at[me], x_recv.at[1]))):
-            spread(ref, sem, j)(r).start()
-        return 0
-
-    lax.fori_loop(1, n, send_last, 0)
+            if pair[0] == N - LEAD:
+                spread(xst, 1)
+
+    spread(x16, 0)
     pl.when(me < owned)(own)
+    all_of(xst, x_recv.at[1])
+    shares_last()
     all_of(x16, x_recv.at[0])
-    all_of(xst, x_recv.at[1])
-    for s, o in enumerate(merge(LAST, lambda j, s, h: x16[j, s, h], [xst[j] for j in range(n)])):
-        o_ref[owned + s] = o.astype(jnp.bfloat16)
+    merge_last()
 
     def blocks(ref, count, sem):
         run = ref.at[pl.ds(0, count)]
@@ -269,6 +290,7 @@
                 pltpu.VMEM((n, halves + 1, ROWS, LANES), f32),
                 pltpu.VMEM((n, LAST, halves, ROWS, head), bf16),
                 pltpu.VMEM((n, ROWS, LANES), f32),
+                pltpu.VMEM((n, LAST, halves, ROWS, LANES), f32),
                 dma(()),
                 dma((KEYS,)),
                 dma((SLOTS,)),

time: 38.1 us -> 37.7 us (0.990)
  no operation moved by 1% of the time
where the time goes in v4:
time: 37.7 us
  Pallas kernels  37 us (98%)
  local copies, waits for them, and re-layouts  0.66 us (2%)
    pallas_call x1, Pallas kernels, step(): pl.pallas_call(functools.partial(kernel, n), out_shape=pltpu.VMEM((N, hal...  37 us

profile of v4, /device:TPU:97, one launch (start us, length us, event | category | flops | bytes accessed | tf_op | source)
XLA Modules:
  0.0 37.7 jit_solution(8835371284406759958)
XLA Ops:
  0.0 37.0 %shard_map.37 = bf16[32,2,8,128]{3,2,1,0:T(8,128)(2,1)S(1)} custom-call(bf16[32,16,128]{2,1,0:T(8,128)(2,1)} %q_hbm.1, bf16[32,4096,128]{2,1,0:T(8,128)(2,1)} %bitcast.4, bf16[32,4096,128]{2,1,0:T(8,128)(2,1)} %bitcast.5), custom_call_target="tpu_custom_call" | custom-call | tf_op jit(solution)/shard_map/pallas_call | solution.py:277
  37.0 0.7 %copy.5 = bf16[32,16,128]{2,1,0:T(8,128)(2,1)} copy(bf16[32,16,128]{2,1,0:T(8,128)(2,1)S(1)} %bitcast.3) | data formatting | bytes 262144
